TPU v7x, 256 devices: a whole 4x4x8 slice. The times are simulated.
256 devices in a mesh: sta: 16 (over z, core), cell: 16 (over x, y).
Axes of the slice: x: 4, y: 4, z: 8, core: 2. Of those that a mesh axis runs over, the one named last changes fastest.
Arguments:
- station_xyz: float32 [3, 4096], P(None, 'sta'), may hold values from 0 to 1, as said below
- cell_xyz: float32 [3, 524288], P(None, 'cell'), may hold values from -0.6 to 1, as said below
- cell_weight: float32 [524288], P('cell'), may hold values from 0.3 to 3
- data: float32 [4096], P(('sta', 'cell')), may hold values from -6 to 6
- model_start: float32 [524288], P(('cell', 'sta')), may hold values from -6 to 6
Outputs:
- model_next: float32 [524288], P(('cell', 'sta'))
- residual_next: float32 [4096], P(('sta', 'cell'))
- search_next: float32 [524288], P(('cell', 'sta'))
Inputs may be any that keep to these rules, and one draw needn't show every extreme that they name: `station_xyz`: rows 0 and 1 lie in [0, 1), row 2 in [0, 0.05]. `cell_xyz`: rows 0 and 1 lie in [0, 1), row 2 in [-0.6, -0.02].
All inputs are finite; a program needn't handle non-finite values.
Results may differ from a plain program's by a relative error of at most 0.0003.
Values sent between devices are 32-bit elements; how exact they have to be, the bound alone decides.
A program may use at most 64 MiB of HBM per device.

v0:
```python
import functools
import math

import jax
import jax.numpy as jnp
from jax import lax
from jax.experimental import pallas as pl
from jax.experimental.pallas import tpu as pltpu
from jax.sharding import Mesh
from jax.sharding import PartitionSpec as P

STA = ("sta_0", "sta_1")
CELL = ("cell_0", "cell_1")
STA_CELL = ("sta_0", "sta_1", "cell_0", "cell_1")
CELL_STA = ("cell_0", "cell_1", "sta_0", "sta_1")

SOFT = 0.0001
LANES = 128
ROWS = 16
PIECE = ROWS * LANES
LOGICAL = pl.DeviceIdType.LOGICAL


def tree_sum(parts):
    while len(parts) > 1:
        parts = [a + b for a, b in zip(parts[::2], parts[1::2])] + parts[len(parts) // 2 * 2 :]
    return parts[0]


def body(
    nz,
    npl,
    half,
    own_len,
    scale,
    sta_ref,
    cel_ref,
    wgt_ref,
    dat_ref,
    mod_ref,
    model_out,
    res_out,
    search_out,
    tile,
    cols,
    acc,
    rcol,
    other,
    w_all,
    v_all,
    m_all,
    p1,
    rs_out,
    rs1,
    g_all,
    p2,
    dl,
    rs2,
    sc1,
    sc2,
    pad,
    send,
    recv,
):
    me = lax.axis_index(STA_CELL)
    z, q = me // npl, me % npl
    core = q // (npl // 2)
    stations = 2 * half
    groups = stations // 8
    srows = stations // LANES

    def plane_peer(d):
        return z * npl + (q + d) % npl

    def z_peer(d):
        return (z + d) % nz * npl + q

    def put(src, dst, sem, peer):
        copy = pltpu.make_async_remote_copy(
            src_ref=src,
            dst_ref=dst,
            send_sem=send.at[sem],
            recv_sem=recv.at[sem],
            device_id=peer,
            device_id_type=LOGICAL,
        )
        copy.start()

    def arrived(ref, sem):
        pltpu.make_async_copy(ref, ref, recv.at[sem]).wait()

    def left(ref, sem):
        pltpu.make_async_copy(ref, ref, send.at[sem]).wait()

    def over_z(buf, sem):
        for d in sorted(range(1, nz), key=lambda d: -min(d, nz - d)):
            put(buf.at[0], buf.at[d], sem, z_peer(d))

    def over_plane(buf, sem):
        for d in range(1, npl):
            put(buf.at[0], buf.at[d], sem, plane_peer(d))

    def others(buf):
        return buf.at[pl.ds(1, buf.shape[0] - 1)]

    barrier = pltpu.get_barrier_semaphore()
    for d in range(1, npl):
        pl.semaphore_signal(barrier, inc=1, device_id=plane_peer(d), device_id_type=LOGICAL)
    for d in range(1, nz):
        pl.semaphore_signal(barrier, inc=1, device_id=z_peer(d), device_id_type=LOGICAL)

    def place(k):
        return (z + nz - k) % nz * 2 + core

    def columns(ref, base):
        for axis in range(3):
            for part in range(half // LANES):
                row = ref[axis : axis + 1, part * LANES : (part + 1) * LANES]
                at = pl.multiple_of(base + part * LANES, LANES)
                cols[axis, pl.ds(at, LANES), :] = jnp.broadcast_to(row, (LANES, LANES)).T

    def generate(base, low, high):
        def step(n, _):
            k = n // (ROWS // 2)
            t = n % (ROWS // 2) * 2
            at = pl.multiple_of(place(k) * PIECE + t * LANES, LANES)
            cell = [
                [
                    jnp.broadcast_to(
                        cel_ref[axis : axis + 1, pl.ds(at + u * LANES, LANES)], (8, LANES)
                    )
                    for axis in range(3)
                ]
                for u in range(2)
            ]

            def group(i, _):
                rows = pl.ds(pl.multiple_of(base + i * 8, 8), 8)
                sx, sy, sz = (cols[axis, rows, :] for axis in range(3))
                for u in range(2):
                    cx, cy, cz = cell[u]
                    dx, dy, dz = sx - cx, sy - cy, sz - cz
                    inv = lax.rsqrt(dx * dx + dy * dy + dz * dz + SOFT)
                    lane = pl.ds(pl.multiple_of((t + u) * LANES, LANES), LANES)
                    tile[k, rows, lane] = dz * inv * (inv * inv)
                return 0

            lax.fori_loop(0, half // 8, group, 0, unroll=4)
            return 0

        lax.fori_loop(low * (ROWS // 2), high * (ROWS // 2), step, 0)

    def weighted(ref):
        v_all[...] = w_all[...] * ref[...]

    def forward():
        acc[...] = jnp.zeros_like(acc)

        def piece(k, _):
            vec = [
                jnp.broadcast_to(v_all[k, t : t + 1, :], (8, LANES)) for t in range(ROWS)
            ]

            def group(i, _):
                rows = pl.ds(pl.multiple_of(i * 8, 8), 8)
                acc[rows, :] += tree_sum(
                    [
                        tile[k, rows, t * LANES : (t + 1) * LANES] * vec[t]
                        for t in range(ROWS)
                    ]
                )
                return 0

            lax.fori_loop(0, groups, group, 0, unroll=4)
            return 0

        lax.fori_loop(0, nz, piece, 0)
        return [
            jnp.sum(acc[s * LANES : (s + 1) * LANES, :].T, axis=0, keepdims=True)
            for s in range(srows)
        ]

    def spread(vec):
        for s in range(srows):
            rcol[s * LANES : (s + 1) * LANES, :] = jnp.broadcast_to(
                vec[s : s + 1, :], (LANES, LANES)
            ).T

    def backward(k):
        def group(i, sums):
            rows = pl.ds(pl.multiple_of(i * 8, 8), 8)
            r = rcol[rows, :]
            return tuple(
                sums[t] + tile[k, rows, t * LANES : (t + 1) * LANES] * r for t in range(ROWS)
            )

        zero = jnp.zeros((8, LANES), jnp.float32)
        sums = lax.fori_loop(0, groups, group, (zero,) * ROWS, unroll=4)
        for t in range(ROWS):
            rs_out[k, t : t + 1, :] = jnp.sum(sums[t], axis=0, keepdims=True)

    def reduce_to_owner(buf, sem):
        order = sorted(range(1, nz), key=lambda d: -min(d, nz - d))
        for k in order:
            backward(k)
            put(rs_out.at[k], buf.at[k], sem, (z + nz - k) % nz * npl + q)
        backward(0)
        arrived(others(buf), sem)
        total = rs_out[0]
        for k in range(1, nz):
            total = total + buf[k]
        left(others(rs_out), sem)
        return w_all[0] * total

    columns(sta_ref, core * half)
    generate(core * half, 0, nz // 2)
    pl.semaphore_wait(barrier, npl - 1 + nz - 1)
    put(sta_ref, other, 0, plane_peer(npl // 2))
    m_all[0] = mod_ref[...]
    for d in sorted(range(1, nz), key=lambda d: -min(d, nz - d)):
        put(mod_ref, m_all.at[d], 1, z_peer(d))
    generate(core * half, nz // 2, nz)
    arrived(other, 0)
    columns(other, (1 - core) * half)
    generate((1 - core) * half, 0, nz)
    for k in range(nz):
        w_all[k] = wgt_ref[place(k)] * scale

    arrived(others(m_all), 1)
    weighted(m_all)
    image = jnp.concatenate(forward(), axis=0)
    pad[...] = jnp.zeros_like(pad)
    pad[0:1, 0:own_len] = dat_ref[...]
    first = q * own_len
    mine = lax.broadcasted_iota(jnp.int32, (srows, LANES), 0) == first // LANES
    own = pltpu.roll(pad[...], first % LANES, 1)[0:1, :]
    p1[0] = jnp.where(mine, own, 0.0) - image
    over_plane(p1, 2)
    arrived(others(p1), 2)
    res = jnp.sum(p1[...], axis=0)

    spread(res)
    grad = reduce_to_owner(rs1, 3)
    g_all[0] = grad
    over_z(g_all, 4)
    arrived(others(g_all), 4)

    grads = g_all[...]
    v_all[...] = w_all[...] * grads
    square = grads * grads
    square = jnp.sum(jnp.sum(square, axis=0), axis=0, keepdims=True)
    rows = forward()
    p2[0] = jnp.concatenate(rows + [square], axis=0)
    over_plane(p2, 5)
    arrived(others(p2), 5)
    total = jnp.sum(p2[...], axis=0)
    image = total[0:srows]
    gamma = jnp.sum(total[srows : srows + 1], axis=1, keepdims=True)
    dl[0] = jnp.sum(image * image, axis=0, keepdims=True)
    over_z(dl, 6)

    spread(image)
    turn = reduce_to_owner(rs2, 7)
    arrived(others(dl), 6)
    delta = jnp.sum(jnp.sum(dl[...], axis=0), axis=1, keepdims=True)
    alpha = gamma / delta
    grad_next = grad - alpha * turn
    sc1[0] = jnp.sum(grad_next * grad_next, axis=0, keepdims=True)
    over_z(sc1, 8)
    model_out[...] = mod_ref[...] + alpha * grad
    res_next = jnp.where(mine, res - alpha * image, 0.0)
    pad[0:1, :] = jnp.sum(res_next, axis=0, keepdims=True)
    res_out[...] = pltpu.roll(pad[...], (LANES - first % LANES) % LANES, 1)[0:1, :]
    arrived(others(sc1), 8)
    sc2[0] = jnp.sum(sc1[...], axis=0)
    over_plane(sc2, 9)
    arrived(others(sc2), 9)
    gamma_next = jnp.sum(jnp.sum(sc2[...], axis=0), axis=1, keepdims=True)
    search_out[...] = grad_next + gamma_next / gamma * grad

    left(other, 0)
    for buf, sem in ((m_all, 1), (p1, 2), (g_all, 4), (p2, 5), (dl, 6), (sc1, 8), (sc2, 9)):
        left(others(buf), sem)


def solution(mesh):
    shape = mesh.devices.shape
    nx = ny = math.isqrt(shape[1])
    nz = shape[0] // 2
    npl = 2 * shape[1]
    torus = Mesh(
        mesh.devices.reshape(nz, 2, nx, ny), ("sta_0", "sta_1", "cell_0", "cell_1")
    )

    def per_device(station_xyz, cell_xyz, cell_weight, data, model_start):
        half = station_xyz.shape[1]
        stations, srows = 2 * half, 2 * half // LANES
        own_len = data.shape[0]
        scale = 1.0 / math.sqrt(half * 2 * nz * cell_xyz.shape[1] * nx * ny)
        vmem = pl.BlockSpec(memory_space=pltpu.VMEM)
        f32 = jnp.float32
        cells = pltpu.VMEM((nz, ROWS, LANES), f32)
        model, res, search = pl.pallas_call(
            functools.partial(body, nz, npl, half, own_len, scale),
            out_shape=(
                jax.ShapeDtypeStruct((ROWS, LANES), f32),
                jax.ShapeDtypeStruct((1, LANES), f32),
                jax.ShapeDtypeStruct((ROWS, LANES), f32),
            ),
            in_specs=[vmem] * 5,
            out_specs=(vmem,) * 3,
            scratch_shapes=[
                pltpu.VMEM((nz, stations, PIECE), f32),
                pltpu.VMEM((3, stations, LANES), f32),
                pltpu.VMEM((stations, LANES), f32),
                pltpu.VMEM((stations, LANES), f32),
                pltpu.VMEM((3, half), f32),
                cells,
                cells,
                cells,
                pltpu.VMEM((npl, srows, LANES), f32),
                cells,
                cells,
                cells,
                pltpu.VMEM((npl, srows + 1, LANES), f32),
                pltpu.VMEM((nz, 1, LANES), f32),
                cells,
                pltpu.VMEM((nz, 1, LANES), f32),
                pltpu.VMEM((npl, 1, LANES), f32),
                pltpu.VMEM((8, LANES), f32),
                pltpu.SemaphoreType.DMA((10,)),
                pltpu.SemaphoreType.DMA((10,)),
            ],
            compiler_params=pltpu.CompilerParams(
                collective_id=0,
                has_side_effects=True,
                vmem_limit_bytes=48 * 1024 * 1024,
            ),
            name="cgls",
        )(
            station_xyz,
            cell_xyz,
            cell_weight.reshape(-1, ROWS, LANES),
            data.reshape(1, own_len),
            model_start.reshape(ROWS, LANES),
        )
        return model.reshape(-1), res[0, :own_len], search.reshape(-1)

    in_specs = (P(None, STA), P(None, CELL), P(CELL), P(STA_CELL), P(CELL_STA))
    out_specs = (P(CELL_STA), P(STA_CELL), P(CELL_STA))
    return jax.shard_map(
        per_device, mesh=torus, in_specs=in_specs, out_specs=out_specs, check_vma=False
    )
```

profile of v0, /device:TPU:1, one launch (start us, length us, event | category | flops | bytes accessed | tf_op | source)
XLA Modules:
  0.0 83.3 jit_solution(5288034094354956895)
XLA Ops:
  0.6 0.0 copy-start.3
  0.6 0.0 copy-start.4
  0.7 0.7 copy-done.3
  1.3 0.0 copy-done.4
  1.3 0.0 copy-start
  1.3 1.0 %copy-done = f32[3,32768]{1,0:T(4,128)S(1)} copy-done((f32[3,32768]{1,0:T(4,128)S(1)}, f32[3,32768]{1,0:T(4,128)}, u32[]{:S(2)}) %copy-start) | copy-done | bytes 393240
  2.4 0.0 copy-start.1
  2.4 0.9 %copy-done.1 = f32[32768]{0:T(1024)S(1)} copy-done((f32[32768]{0:T(1024)S(1)}, f32[32768]{0:T(1024)}, u32[]{:S(2)}) %copy-start.1) | copy-done | bytes 131096
  3.3 0.0 copy-start.2
  3.3 0.7 copy-done.2
  4.0 77.6 %cgls.1 = (f32[16,128]{1,0:T(8,128)S(1)}, f32[1,128]{1,0:T(1,128)S(1)}, f32[16,128]{1,0:T(8,128)S(1)}) custom-call(f32[3,256]{1,0:T(4,128)S(1)} %copy-done.3, f32[3,32768]{1,0:T(4,128)S(1)} %copy-done, f32[16,16,128]{2,1,0:T(8,128)S(1)} %bitcast.7, f32[1,16]{1,0:T(1,128)S(1)} %bitcast.11, f32[16,128]{1,0:T(8,128)S(1)} %bitcast.8), custom_call_target="tpu_custom_call" | custom-call | tf_op jit(solution)/shard_map/cgls/pallas_call | solution.py:303
  81.6 0.5 slice_bitcast_fusion
  82.1 0.6 copy.10
  82.7 0.6 copy.11
Async XLA Ops:
  0.6 0.7 copy-start.3
  0.6 0.7 copy-start.4
  1.3 1.0 %copy-start = (f32[3,32768]{1,0:T(4,128)S(1)}, f32[3,32768]{1,0:T(4,128)}, u32[]{:S(2)}) copy-start(f32[3,32768]{1,0:T(4,128)} %cel_ref.1) | copy-start | bytes 1179652
  2.4 0.9 %copy-start.1 = (f32[32768]{0:T(1024)S(1)}, f32[32768]{0:T(1024)}, u32[]{:S(2)}) copy-start(f32[32768]{0:T(1024)} %param.7) | copy-start | bytes 393220
  3.3 0.7 copy-start.2
where the time goes:
time: 83.5 us; the launch traced here: 83.3 us
  Pallas kernels  77.6 us (93%)
  local copies, waits for them, and re-layouts  5.03 us (6%)
    pallas_call x1, Pallas kernels, per_device(): pl.pallas_call(functools.partial(body, nz, npl, half, own_len, scale), ou...  77.6 us
    unnamed x12, local copies, waits for them, and re-layouts  4.51 us

commit v1 on v0

--- a/solution.py
+++ b/solution.py
@@ -15,6 +15,8 @@
 CELL_STA = ("cell_0", "cell_1", "sta_0", "sta_1")
 
 SOFT = 0.0001
+MID_XY = 0.5
+MID_Z = -0.275
 LANES = 128
 ROWS = 16
 PIECE = ROWS * LANES
@@ -42,10 +44,18 @@
     res_out,
     search_out,
     tile,
-    cols,
+    lhs,
+    rhs,
+    near,
+    far,
+    x_pad,
+    z_col,
     acc,
     rcol,
+    sta,
     other,
+    cel,
+    dat,
     w_all,
     v_all,
     m_all,
@@ -61,6 +71,8 @@
     pad,
     send,
     recv,
+    pieces,
+    load,
 ):
     me = lax.axis_index(STA_CELL)
     z, q = me // npl, me % npl
@@ -75,12 +87,12 @@
     def z_peer(d):
         return (z + d) % nz * npl + q
 
-    def put(src, dst, sem, peer):
+    def put(src, dst, sem, peer, landed=None):
         copy = pltpu.make_async_remote_copy(
             src_ref=src,
             dst_ref=dst,
             send_sem=send.at[sem],
-            recv_sem=recv.at[sem],
+            recv_sem=recv.at[sem] if landed is None else landed,
             device_id=peer,
             device_id_type=LOGICAL,
         )
@@ -92,9 +104,10 @@
     def left(ref, sem):
         pltpu.make_async_copy(ref, ref, send.at[sem]).wait()
 
-    def over_z(buf, sem):
+    def over_z(buf, sem, group=None):
         for d in sorted(range(1, nz), key=lambda d: -min(d, nz - d)):
-            put(buf.at[0], buf.at[d], sem, z_peer(d))
+            landed = None if group is None else pieces.at[group, d]
+            put(buf.at[0], buf.at[d], sem, z_peer(d), landed)
 
     def over_plane(buf, sem):
         for d in range(1, npl):
@@ -109,59 +122,90 @@
     for d in range(1, nz):
         pl.semaphore_signal(barrier, inc=1, device_id=z_peer(d), device_id_type=LOGICAL)
 
+    loads = [pltpu.make_async_copy(sta_ref, sta, load.at[0])]
     def place(k):
         return (z + nz - k) % nz * 2 + core
 
-    def columns(ref, base):
-        for axis in range(3):
-            for part in range(half // LANES):
-                row = ref[axis : axis + 1, part * LANES : (part + 1) * LANES]
-                at = pl.multiple_of(base + part * LANES, LANES)
-                cols[axis, pl.ds(at, LANES), :] = jnp.broadcast_to(row, (LANES, LANES)).T
+    for k in range(nz):
+        at = pl.ds(pl.multiple_of(place(k) * PIECE, PIECE), PIECE)
+        loads.append(pltpu.make_async_copy(cel_ref.at[:, at], cel.at[k], load.at[1 + k]))
+    for k in range(nz):
+        loads.append(pltpu.make_async_copy(wgt_ref.at[place(k)], w_all.at[k], load.at[1 + nz + k]))
+    loads.append(pltpu.make_async_copy(mod_ref, m_all.at[0], load.at[1 + 2 * nz]))
+    loads.append(pltpu.make_async_copy(dat_ref, dat, load.at[2 + 2 * nz]))
+
+    def split(x):
+        high = x.astype(jnp.bfloat16).astype(jnp.float32)
+        rest = x - high
+        mid = rest.astype(jnp.bfloat16).astype(jnp.float32)
+        return high, mid, rest - mid
+
+    def station_side(ref, base):
+        axis = lax.broadcasted_iota(jnp.int32, (3, half), 0)
+        s = ref[...] - jnp.where(axis == 2, MID_Z, MID_XY)
+        high, mid, low = (-2.0 * part for part in split(s))
+        length = split(jnp.sum(s * s, axis=0, keepdims=True))
+        one = jnp.ones((1, half), jnp.float32)
+        zero = jnp.zeros((1, half), jnp.float32)
+        rows = [high, one, *length, one, high, one, mid, zero]
+        rows += [mid, zero, high, zero, low, zero, mid, zero]
+        lhs[pl.ds(base, half), :] = jnp.concatenate(rows, axis=0).T.astype(jnp.bfloat16)
+        for part in range(half // LANES):
+            row = ref[2:3, part * LANES : (part + 1) * LANES]
+            at = pl.multiple_of(base + part * LANES, LANES)
+            z_col[pl.ds(at, LANES), :] = jnp.broadcast_to(row, (LANES, LANES)).T
+
+    def cell_side(k, _):
+        x_pad[0:3, :] = cel[k]
+        x_pad[4:7, :] = cel[k]
+        row = lax.broadcasted_iota(jnp.int32, (8, PIECE), 0)
+        mid_of = jnp.where(row % 4 == 2, MID_Z, jnp.where(row % 4 == 3, 0.0, MID_XY))
+        x = x_pad[...] - mid_of
+        square = x * x
+        square = square + pltpu.roll(square, 1, 0)
+        high, mid, low = split(x)
+        length = split(square + pltpu.roll(square, 2, 0))
+        first = row < 4
+        last = row % 4 == 3
+        parts = [
+            jnp.where(last, jnp.where(first, length[0], length[1]), jnp.where(first, high, 1.0)),
+            jnp.where(first, jnp.where(last, length[2], mid), high),
+            jnp.where(first, mid, low),
+            jnp.where(first, high, low),
+        ]
+        rhs[k] = jnp.concatenate(parts, axis=0).astype(jnp.bfloat16)
+        return 0
+
+    def distances(k, base, buf):
+        buf[...] = jnp.dot(lhs[pl.ds(base, half), :], rhs[k], preferred_element_type=jnp.float32)
+
+    def kernel_of(k, base, buf):
+        for t in range(ROWS):
+            lanes = slice(t * LANES, (t + 1) * LANES)
+            dz = z_col[pl.ds(base, half), :] - cel[k, 2:3, lanes]
+            inv = lax.rsqrt(buf[:, lanes])
+            tile[k, pl.ds(base, half), lanes] = (dz * inv) * (inv * inv)
 
     def generate(base, low, high):
-        def step(n, _):
-            k = n // (ROWS // 2)
-            t = n % (ROWS // 2) * 2
-            at = pl.multiple_of(place(k) * PIECE + t * LANES, LANES)
-            cell = [
-                [
-                    jnp.broadcast_to(
-                        cel_ref[axis : axis + 1, pl.ds(at + u * LANES, LANES)], (8, LANES)
-                    )
-                    for axis in range(3)
-                ]
-                for u in range(2)
-            ]
-
-            def group(i, _):
-                rows = pl.ds(pl.multiple_of(base + i * 8, 8), 8)
-                sx, sy, sz = (cols[axis, rows, :] for axis in range(3))
-                for u in range(2):
-                    cx, cy, cz = cell[u]
-                    dx, dy, dz = sx - cx, sy - cy, sz - cz
-                    inv = lax.rsqrt(dx * dx + dy * dy + dz * dz + SOFT)
-                    lane = pl.ds(pl.multiple_of((t + u) * LANES, LANES), LANES)
-                    tile[k, rows, lane] = dz * inv * (inv * inv)
-                return 0
-
-            lax.fori_loop(0, half // 8, group, 0, unroll=4)
+        def pair(j, _):
+            distances(2 * j + 1, base, far)
+            kernel_of(2 * j, base, near)
+            distances((2 * j + 2) % nz, base, near)
+            kernel_of(2 * j + 1, base, far)
             return 0
 
-        lax.fori_loop(low * (ROWS // 2), high * (ROWS // 2), step, 0)
-
-    def weighted(ref):
-        v_all[...] = w_all[...] * ref[...]
-
-    def forward():
+        lax.fori_loop(low // 2, high // 2, pair, 0)
+
+    near_first = sorted(range(1, nz), key=lambda d: min(d, nz - d))
+
+    def forward(vector):
         acc[...] = jnp.zeros_like(acc)
-
-        def piece(k, _):
-            vec = [
-                jnp.broadcast_to(v_all[k, t : t + 1, :], (8, LANES)) for t in range(ROWS)
-            ]
-
-            def group(i, _):
+        for k in (0, *near_first):
+            value = vector(k)
+            v_all[...] = w_all[k] * value
+            vec = [jnp.broadcast_to(v_all[t : t + 1, :], (8, LANES)) for t in range(ROWS)]
+
+            def group(i, _, k=k, vec=vec):
                 rows = pl.ds(pl.multiple_of(i * 8, 8), 8)
                 acc[rows, :] += tree_sum(
                     [
@@ -171,14 +215,19 @@
                 )
                 return 0
 
-            lax.fori_loop(0, groups, group, 0, unroll=4)
-            return 0
-
-        lax.fori_loop(0, nz, piece, 0)
+            lax.fori_loop(0, groups, group, 0, unroll=16)
         return [
             jnp.sum(acc[s * LANES : (s + 1) * LANES, :].T, axis=0, keepdims=True)
             for s in range(srows)
         ]
+
+    def taken(buf, group):
+        def vector(k):
+            if k:
+                pltpu.make_async_copy(buf.at[k], buf.at[k], pieces.at[group, k]).wait()
+            return buf[k]
+
+        return vector
 
     def spread(vec):
         for s in range(srows):
@@ -195,7 +244,7 @@
             )
 
         zero = jnp.zeros((8, LANES), jnp.float32)
-        sums = lax.fori_loop(0, groups, group, (zero,) * ROWS, unroll=4)
+        sums = lax.fori_loop(0, groups, group, (zero,) * ROWS, unroll=16)
         for t in range(ROWS):
             rs_out[k, t : t + 1, :] = jnp.sum(sums[t], axis=0, keepdims=True)
 
@@ -212,25 +261,34 @@
         left(others(rs_out), sem)
         return w_all[0] * total
 
-    columns(sta_ref, core * half)
-    generate(core * half, 0, nz // 2)
+    for copy in loads:
+        copy.start()
+    x_pad[3:4, :] = jnp.full((1, PIECE), math.sqrt(SOFT), jnp.float32)
+    x_pad[7:8, :] = jnp.full((1, PIECE), math.sqrt(SOFT), jnp.float32)
+    base = pl.multiple_of(core * half, half)
+    loads[0].wait()
+    station_side(sta, base)
+    for copy in loads[1 : 1 + nz]:
+        copy.wait()
+    lax.fori_loop(0, nz, cell_side, 0)
+    distances(0, base, near)
+    generate(base, 0, nz // 2)
+    for copy in loads[1 + nz :]:
+        copy.wait()
     pl.semaphore_wait(barrier, npl - 1 + nz - 1)
-    put(sta_ref, other, 0, plane_peer(npl // 2))
-    m_all[0] = mod_ref[...]
-    for d in sorted(range(1, nz), key=lambda d: -min(d, nz - d)):
-        put(mod_ref, m_all.at[d], 1, z_peer(d))
-    generate(core * half, nz // 2, nz)
+    put(sta, other, 0, plane_peer(npl // 2))
+    over_z(m_all, 1, 0)
+    generate(base, nz // 2, nz)
     arrived(other, 0)
-    columns(other, (1 - core) * half)
-    generate((1 - core) * half, 0, nz)
-    for k in range(nz):
-        w_all[k] = wgt_ref[place(k)] * scale
-
-    arrived(others(m_all), 1)
-    weighted(m_all)
-    image = jnp.concatenate(forward(), axis=0)
+    base = pl.multiple_of((1 - core) * half, half)
+    station_side(other, base)
+    distances(0, base, near)
+    generate(base, 0, nz)
+    w_all[...] = w_all[...] * scale
+
+    image = jnp.concatenate(forward(taken(m_all, 0)), axis=0)
     pad[...] = jnp.zeros_like(pad)
-    pad[0:1, 0:own_len] = dat_ref[...]
+    pad[0:1, 0:own_len] = dat[...]
     first = q * own_len
     mine = lax.broadcasted_iota(jnp.int32, (srows, LANES), 0) == first // LANES
     own = pltpu.roll(pad[...], first % LANES, 1)[0:1, :]
@@ -242,14 +300,11 @@
     spread(res)
     grad = reduce_to_owner(rs1, 3)
     g_all[0] = grad
-    over_z(g_all, 4)
-    arrived(others(g_all), 4)
-
+    over_z(g_all, 4, 1)
+
+    rows = forward(taken(g_all, 1))
     grads = g_all[...]
-    v_all[...] = w_all[...] * grads
-    square = grads * grads
-    square = jnp.sum(jnp.sum(square, axis=0), axis=0, keepdims=True)
-    rows = forward()
+    square = jnp.sum(jnp.sum(grads * grads, axis=0), axis=0, keepdims=True)
     p2[0] = jnp.concatenate(rows + [square], axis=0)
     over_plane(p2, 5)
     arrived(others(p2), 5)
@@ -267,7 +322,7 @@
     grad_next = grad - alpha * turn
     sc1[0] = jnp.sum(grad_next * grad_next, axis=0, keepdims=True)
     over_z(sc1, 8)
-    model_out[...] = mod_ref[...] + alpha * grad
+    model_out[...] = m_all[0] + alpha * grad
     res_next = jnp.where(mine, res - alpha * image, 0.0)
     pad[0:1, :] = jnp.sum(res_next, axis=0, keepdims=True)
     res_out[...] = pltpu.roll(pad[...], (LANES - first % LANES) % LANES, 1)[0:1, :]
@@ -307,16 +362,24 @@
                 jax.ShapeDtypeStruct((1, LANES), f32),
                 jax.ShapeDtypeStruct((ROWS, LANES), f32),
             ),
-            in_specs=[vmem] * 5,
+            in_specs=[pl.BlockSpec(memory_space=pltpu.HBM)] * 5,
             out_specs=(vmem,) * 3,
             scratch_shapes=[
                 pltpu.VMEM((nz, stations, PIECE), f32),
-                pltpu.VMEM((3, stations, LANES), f32),
+                pltpu.VMEM((stations, 32), jnp.bfloat16),
+                pltpu.VMEM((nz, 32, PIECE), jnp.bfloat16),
+                pltpu.VMEM((half, PIECE), f32),
+                pltpu.VMEM((half, PIECE), f32),
+                pltpu.VMEM((8, PIECE), f32),
+                pltpu.VMEM((stations, LANES), f32),
                 pltpu.VMEM((stations, LANES), f32),
                 pltpu.VMEM((stations, LANES), f32),
                 pltpu.VMEM((3, half), f32),
-                cells,
-                cells,
+                pltpu.VMEM((3, half), f32),
+                pltpu.VMEM((nz, 3, PIECE), f32),
+                pltpu.VMEM((1, own_len), f32),
+                cells,
+                pltpu.VMEM((ROWS, LANES), f32),
                 cells,
                 pltpu.VMEM((npl, srows, LANES), f32),
                 cells,
@@ -330,11 +393,13 @@
                 pltpu.VMEM((8, LANES), f32),
                 pltpu.SemaphoreType.DMA((10,)),
                 pltpu.SemaphoreType.DMA((10,)),
+                pltpu.SemaphoreType.DMA((2, nz)),
+                pltpu.SemaphoreType.DMA((2 * nz + 3,)),
             ],
             compiler_params=pltpu.CompilerParams(
                 collective_id=0,
                 has_side_effects=True,
-                vmem_limit_bytes=48 * 1024 * 1024,
+                vmem_limit_bytes=56 * 1024 * 1024,
             ),
             name="cgls",
         )(

time: 83.5 us -> 60.7 us (0.73)
  Pallas kernels: 77.6 us -> 57.4 us
  local copies, waits for them, and re-layouts: 5.03 us -> 2.41 us
    pallas_call x1, Pallas kernels: 77.6 us -> 57.4 us  [per_device(): pl.pallas_call(functools.partial(body, nz, npl, half, own_len, scale), ou...]
    unnamed x12 -> x8, local copies, waits for them, and re-layouts: 4.51 us -> 1.9 us
where the time goes in v1:
time: 60.7 us; the launch traced here: 60.5 us
  Pallas kernels  57.4 us (95%)
  local copies, waits for them, and re-layouts  2.41 us (4%)
  between operations  0.66 us (1%)
    pallas_call x1, Pallas kernels, per_device(): pl.pallas_call(functools.partial(body, nz, npl, half, own_len, scale), ou...  57.4 us
    unnamed x8, local copies, waits for them, and re-layouts  1.9 us

profile of v1, /device:TPU:1, one launch (start us, length us, event | category | flops | bytes accessed | tf_op | source)
XLA Modules:
  0.0 60.5 jit_solution(6007671930431662058)
XLA Ops:
  0.6 57.4 %cgls.1 = (f32[16,128]{1,0:T(8,128)}, f32[1,128]{1,0:T(1,128)}, f32[16,128]{1,0:T(8,128)}) custom-call(f32[3,256]{1,0:T(4,128)} %sta_ref.1, f32[3,32768]{1,0:T(4,128)} %cel_ref.1, f32[16,16,128]{2,1,0:T(8,128)} %bitcast.7, f32[1,16]{1,0:T(1,128)} %bitcast.11, f32[16,128]{1,0:T(8,128)} %bitcast.8), custom_call_target="tpu_custom_call" | custom-call | tf_op jit(solution)/shard_map/cgls/pallas_call | solution.py:358
  58.0 0.0 copy-start.1
  58.0 0.0 copy-start.2
  58.0 0.6 copy-done.2
  58.6 0.5 slice_bitcast_fusion
  59.1 0.0 copy-done.1
  59.2 0.0 copy-start
  59.2 0.6 copy.10
  59.8 0.1 copy-done
  59.9 0.6 copy.11
Async XLA Ops:
  58.0 1.1 %copy-start.1 = (f32[16,128]{1,0:T(8,128)S(1)}, f32[16,128]{1,0:T(8,128)}, u32[]{:S(2)}) copy-start(f32[16,128]{1,0:T(8,128)} %get-tuple-element.6) | copy-start | bytes 24580
  58.0 0.6 copy-start.2
  59.2 0.7 %copy-start = (f32[16,128]{1,0:T(8,128)S(1)}, f32[16,128]{1,0:T(8,128)}, u32[]{:S(2)}) copy-start(f32[16,128]{1,0:T(8,128)} %get-tuple-element.8) | copy-start | bytes 24580

commit v2 on v1

--- a/solution.py
+++ b/solution.py
@@ -31,7 +31,8 @@
 
 def body(
     nz,
-    npl,
+    nx,
+    ny,
     half,
     own_len,
     scale,
@@ -74,15 +75,24 @@
     pieces,
     load,
 ):
+    npl = 2 * nx * ny
     me = lax.axis_index(STA_CELL)
     z, q = me // npl, me % npl
-    core = q // (npl // 2)
+    core = q // (nx * ny)
     stations = 2 * half
     groups = stations // 8
     srows = stations // LANES
 
     def plane_peer(d):
-        return z * npl + (q + d) % npl
+        x, y = q // ny % nx, q % ny
+        to_x, to_y = (x + d // ny % nx) % nx, (y + d % ny) % ny
+        return z * npl + ((core + d // (nx * ny)) % 2 * nx + to_x) * ny + to_y
+
+    def plane_hops(d):
+        dx, dy = d // ny % nx, d % ny
+        return min(dx, nx - dx) + min(dy, ny - dy), d // (nx * ny)
+
+    far_first = sorted(range(1, npl), key=plane_hops, reverse=True)
 
     def z_peer(d):
         return (z + d) % nz * npl + q
@@ -110,17 +120,11 @@
             put(buf.at[0], buf.at[d], sem, z_peer(d), landed)
 
     def over_plane(buf, sem):
-        for d in range(1, npl):
+        for d in far_first:
             put(buf.at[0], buf.at[d], sem, plane_peer(d))
 
     def others(buf):
         return buf.at[pl.ds(1, buf.shape[0] - 1)]
-
-    barrier = pltpu.get_barrier_semaphore()
-    for d in range(1, npl):
-        pl.semaphore_signal(barrier, inc=1, device_id=plane_peer(d), device_id_type=LOGICAL)
-    for d in range(1, nz):
-        pl.semaphore_signal(barrier, inc=1, device_id=z_peer(d), device_id_type=LOGICAL)
 
     loads = [pltpu.make_async_copy(sta_ref, sta, load.at[0])]
     def place(k):
@@ -155,12 +159,12 @@
             at = pl.multiple_of(base + part * LANES, LANES)
             z_col[pl.ds(at, LANES), :] = jnp.broadcast_to(row, (LANES, LANES)).T
 
-    def cell_side(k, _):
-        x_pad[0:3, :] = cel[k]
-        x_pad[4:7, :] = cel[k]
+    def cell_side(k):
+        x_pad[k % 2, 0:3, :] = cel[k]
+        x_pad[k % 2, 4:7, :] = cel[k]
         row = lax.broadcasted_iota(jnp.int32, (8, PIECE), 0)
         mid_of = jnp.where(row % 4 == 2, MID_Z, jnp.where(row % 4 == 3, 0.0, MID_XY))
-        x = x_pad[...] - mid_of
+        x = x_pad[k % 2] - mid_of
         square = x * x
         square = square + pltpu.roll(square, 1, 0)
         high, mid, low = split(x)
@@ -174,7 +178,6 @@
             jnp.where(first, high, low),
         ]
         rhs[k] = jnp.concatenate(parts, axis=0).astype(jnp.bfloat16)
-        return 0
 
     def distances(k, base, buf):
         buf[...] = jnp.dot(lhs[pl.ds(base, half), :], rhs[k], preferred_element_type=jnp.float32)
@@ -186,15 +189,12 @@
             inv = lax.rsqrt(buf[:, lanes])
             tile[k, pl.ds(base, half), lanes] = (dz * inv) * (inv * inv)
 
-    def generate(base, low, high):
-        def pair(j, _):
-            distances(2 * j + 1, base, far)
-            kernel_of(2 * j, base, near)
-            distances((2 * j + 2) % nz, base, near)
-            kernel_of(2 * j + 1, base, far)
-            return 0
-
-        lax.fori_loop(low // 2, high // 2, pair, 0)
+    def generate(base, first, count, after):
+        bufs = (near, far)
+        for i in range(count):
+            ahead = (first + i + 1, base) if i < count - 1 else after
+            distances(*ahead, bufs[(i + 1) % 2])
+            kernel_of(first + i, base, bufs[i % 2])
 
     near_first = sorted(range(1, nz), key=lambda d: min(d, nz - d))
 
@@ -263,27 +263,39 @@
 
     for copy in loads:
         copy.start()
-    x_pad[3:4, :] = jnp.full((1, PIECE), math.sqrt(SOFT), jnp.float32)
-    x_pad[7:8, :] = jnp.full((1, PIECE), math.sqrt(SOFT), jnp.float32)
+    barrier = pltpu.get_barrier_semaphore()
+    for d in range(1, npl):
+        pl.semaphore_signal(barrier, inc=1, device_id=plane_peer(d), device_id_type=LOGICAL)
+    for d in range(1, nz):
+        pl.semaphore_signal(barrier, inc=1, device_id=z_peer(d), device_id_type=LOGICAL)
+    for i in range(2):
+        for row in (3, 7):
+            x_pad[i, row : row + 1, :] = jnp.full((1, PIECE), math.sqrt(SOFT), jnp.float32)
     base = pl.multiple_of(core * half, half)
-    loads[0].wait()
+    for copy in loads[: 1 + nz]:
+        copy.wait()
     station_side(sta, base)
-    for copy in loads[1 : 1 + nz]:
-        copy.wait()
-    lax.fori_loop(0, nz, cell_side, 0)
+    cell_side(0)
     distances(0, base, near)
-    generate(base, 0, nz // 2)
+    for k in range(1, nz):
+        cell_side(k)
+    generate(base, 0, nz // 2, (nz // 2, base))
     for copy in loads[1 + nz :]:
         copy.wait()
     pl.semaphore_wait(barrier, npl - 1 + nz - 1)
-    put(sta, other, 0, plane_peer(npl // 2))
+    put(sta, other, 0, plane_peer(nx * ny))
     over_z(m_all, 1, 0)
-    generate(base, nz // 2, nz)
+    base_2 = pl.multiple_of((1 - core) * half, half)
+    generate(base, nz // 2, nz // 4, (nz // 2 + nz // 4, base))
     arrived(other, 0)
-    base = pl.multiple_of((1 - core) * half, half)
-    station_side(other, base)
-    distances(0, base, near)
-    generate(base, 0, nz)
+    station_side(other, base_2)
+    generate(base, nz // 2 + nz // 4, nz // 4, (0, base_2))
+
+    def half_of(j, _):
+        generate(base_2, j * (nz // 2), nz // 2, ((j + 1) % 2 * (nz // 2), base_2))
+        return 0
+
+    lax.fori_loop(0, 2, half_of, 0)
     w_all[...] = w_all[...] * scale
 
     image = jnp.concatenate(forward(taken(m_all, 0)), axis=0)
@@ -325,7 +337,7 @@
     model_out[...] = m_all[0] + alpha * grad
     res_next = jnp.where(mine, res - alpha * image, 0.0)
     pad[0:1, :] = jnp.sum(res_next, axis=0, keepdims=True)
-    res_out[...] = pltpu.roll(pad[...], (LANES - first % LANES) % LANES, 1)[0:1, :]
+    res_out[...] = pltpu.roll(pad[...], (LANES - first % LANES) % LANES, 1)[0:1, :own_len]
     arrived(others(sc1), 8)
     sc2[0] = jnp.sum(sc1[...], axis=0)
     over_plane(sc2, 9)
@@ -338,14 +350,24 @@
         left(others(buf), sem)
 
 
+def write_out(model, res, search, model_out, res_out, search_out, sem):
+    pairs = ((model, model_out), (res, res_out), (search, search_out))
+    copies = [pltpu.make_async_copy(a, b, sem.at[i]) for i, (a, b) in enumerate(pairs)]
+    for copy in copies:
+        copy.start()
+    for copy in copies:
+        copy.wait()
+
+
 def solution(mesh):
     shape = mesh.devices.shape
     nx = ny = math.isqrt(shape[1])
     nz = shape[0] // 2
-    npl = 2 * shape[1]
     torus = Mesh(
         mesh.devices.reshape(nz, 2, nx, ny), ("sta_0", "sta_1", "cell_0", "cell_1")
     )
+
+    npl = 2 * shape[1]
 
     def per_device(station_xyz, cell_xyz, cell_weight, data, model_start):
         half = station_xyz.shape[1]
@@ -355,13 +377,14 @@
         vmem = pl.BlockSpec(memory_space=pltpu.VMEM)
         f32 = jnp.float32
         cells = pltpu.VMEM((nz, ROWS, LANES), f32)
-        model, res, search = pl.pallas_call(
-            functools.partial(body, nz, npl, half, own_len, scale),
-            out_shape=(
-                jax.ShapeDtypeStruct((ROWS, LANES), f32),
-                jax.ShapeDtypeStruct((1, LANES), f32),
-                jax.ShapeDtypeStruct((ROWS, LANES), f32),
-            ),
+        shapes = (
+            jax.ShapeDtypeStruct((ROWS, LANES), f32),
+            jax.ShapeDtypeStruct((1, own_len), f32),
+            jax.ShapeDtypeStruct((ROWS, LANES), f32),
+        )
+        results = pl.pallas_call(
+            functools.partial(body, nz, nx, ny, half, own_len, scale),
+            out_shape=tuple(pltpu.VMEM(x.shape, x.dtype) for x in shapes),
             in_specs=[pl.BlockSpec(memory_space=pltpu.HBM)] * 5,
             out_specs=(vmem,) * 3,
             scratch_shapes=[
@@ -370,7 +393,7 @@
                 pltpu.VMEM((nz, 32, PIECE), jnp.bfloat16),
                 pltpu.VMEM((half, PIECE), f32),
                 pltpu.VMEM((half, PIECE), f32),
-                pltpu.VMEM((8, PIECE), f32),
+                pltpu.VMEM((2, 8, PIECE), f32),
                 pltpu.VMEM((stations, LANES), f32),
                 pltpu.VMEM((stations, LANES), f32),
                 pltpu.VMEM((stations, LANES), f32),
@@ -409,7 +432,15 @@
             data.reshape(1, own_len),
             model_start.reshape(ROWS, LANES),
         )
-        return model.reshape(-1), res[0, :own_len], search.reshape(-1)
+        model, res, search = pl.pallas_call(
+            write_out,
+            out_shape=shapes,
+            in_specs=[vmem] * 3,
+            out_specs=(pl.BlockSpec(memory_space=pltpu.HBM),) * 3,
+            scratch_shapes=[pltpu.SemaphoreType.DMA((3,))],
+            name="write_out",
+        )(*(pltpu.with_memory_space_constraint(x, pltpu.VMEM) for x in results))
+        return model.reshape(-1), res.reshape(-1), search.reshape(-1)
 
     in_specs = (P(None, STA), P(None, CELL), P(CELL), P(STA_CELL), P(CELL_STA))
     out_specs = (P(CELL_STA), P(STA_CELL), P(CELL_STA))

time: 60.7 us -> 56.4 us (0.929)
  local copies, waits for them, and re-layouts: 2.41 us -> 0 us
  Pallas kernels: 57.4 us -> 55.6 us
    unnamed x8 -> x0, local copies, waits for them, and re-layouts: 1.9 us -> none
    pallas_call x1 -> x2, Pallas kernels: 57.4 us -> 55.6 us  [the longest x1 55 us: per_device(): pl.pallas_call(functools.partial(body, nz, nx, ny, half, own_len, scale),...]
where the time goes in v2:
time: 56.4 us; the launch traced here: 56.2 us
  Pallas kernels  55.6 us (99%)
  between operations  0.64 us (1%)
    pallas_call x1, Pallas kernels, per_device(): pl.pallas_call(functools.partial(body, nz, nx, ny, half, own_len, scale),...  55 us

profile of v2, /device:TPU:1, one launch (start us, length us, event | category | flops | bytes accessed | tf_op | source)
XLA Modules:
  0.0 56.2 jit_solution(3237829059925020725)
XLA Ops:
  0.6 55.0 %cgls.1 = (f32[16,128]{1,0:T(8,128)S(1)}, f32[1,16]{1,0:T(1,128)S(1)}, f32[16,128]{1,0:T(8,128)S(1)}) custom-call(f32[3,256]{1,0:T(4,128)} %sta_ref.1, f32[3,32768]{1,0:T(4,128)} %cel_ref.1, f32[16,16,128]{2,1,0:T(8,128)} %bitcast.6, f32[1,16]{1,0:T(1,128)} %bitcast.8, f32[16,128]{1,0:T(8,128)} %bitcast.7), custom_call_target="tpu_custom_call" | custom-call | tf_op jit(solution)/shard_map/cgls/pallas_call | solution.py:385
  55.6 0.6 %write_out.1 = (f32[16,128]{1,0:T(8,128)}, f32[1,16]{1,0:T(1,128)}, f32[16,128]{1,0:T(8,128)}) custom-call(f32[16,128]{1,0:T(8,128)S(1)} %get-tuple-element.9.model, f32[1,16]{1,0:T(1,128)S(1)} %get-tuple-element.10.res, f32[16,128]{1,0:T(8,128)S(1)} %get-tuple-element.11.search), custom_call_target="tpu_custom_call" | custom-call | tf_op jit(solution)/shard_map/write_out/pallas_call | solution.py:435

commit v3 on v2

--- a/solution.py
+++ b/solution.py
@@ -67,8 +67,7 @@
     p2,
     dl,
     rs2,
-    sc1,
-    sc2,
+    sc,
     pad,
     send,
     recv,
@@ -332,21 +331,22 @@
     delta = jnp.sum(jnp.sum(dl[...], axis=0), axis=1, keepdims=True)
     alpha = gamma / delta
     grad_next = grad - alpha * turn
-    sc1[0] = jnp.sum(grad_next * grad_next, axis=0, keepdims=True)
-    over_z(sc1, 8)
+    sc[0] = jnp.sum(grad_next * grad_next, axis=0, keepdims=True)
+    for dz in (*reversed(near_first), 0):
+        for d in (*far_first, 0):
+            if dz or d:
+                peer = (z + dz) % nz * npl + plane_peer(d) - z * npl
+                put(sc.at[0], sc.at[dz * npl + d], 8, peer)
     model_out[...] = m_all[0] + alpha * grad
     res_next = jnp.where(mine, res - alpha * image, 0.0)
     pad[0:1, :] = jnp.sum(res_next, axis=0, keepdims=True)
     res_out[...] = pltpu.roll(pad[...], (LANES - first % LANES) % LANES, 1)[0:1, :own_len]
-    arrived(others(sc1), 8)
-    sc2[0] = jnp.sum(sc1[...], axis=0)
-    over_plane(sc2, 9)
-    arrived(others(sc2), 9)
-    gamma_next = jnp.sum(jnp.sum(sc2[...], axis=0), axis=1, keepdims=True)
+    arrived(others(sc), 8)
+    gamma_next = jnp.sum(jnp.sum(sc[...], axis=0), axis=1, keepdims=True)
     search_out[...] = grad_next + gamma_next / gamma * grad
 
     left(other, 0)
-    for buf, sem in ((m_all, 1), (p1, 2), (g_all, 4), (p2, 5), (dl, 6), (sc1, 8), (sc2, 9)):
+    for buf, sem in ((m_all, 1), (p1, 2), (g_all, 4), (p2, 5), (dl, 6), (sc, 8)):
         left(others(buf), sem)
 
 
@@ -411,8 +411,7 @@
                 pltpu.VMEM((npl, srows + 1, LANES), f32),
                 pltpu.VMEM((nz, 1, LANES), f32),
                 cells,
-                pltpu.VMEM((nz, 1, LANES), f32),
-                pltpu.VMEM((npl, 1, LANES), f32),
+                pltpu.VMEM((nz * npl, 1, LANES), f32),
                 pltpu.VMEM((8, LANES), f32),
                 pltpu.SemaphoreType.DMA((10,)),
                 pltpu.SemaphoreType.DMA((10,)),

time: 56.4 us -> 54.7 us (0.970)
  Pallas kernels: 55.6 us -> 53.9 us
    pallas_call x1, Pallas kernels: 55 us -> 53.3 us  [per_device(): pl.pallas_call(functools.partial(body, nz, nx, ny, half, own_len, scale),...]
where the time goes in v3:
time: 54.7 us; the launch traced here: 54.5 us
  Pallas kernels  53.9 us (99%)
  between operations  0.64 us (1%)
    pallas_call x1, Pallas kernels, per_device(): pl.pallas_call(functools.partial(body, nz, nx, ny, half, own_len, scale),...  53.3 us

profile of v3, /device:TPU:1, one launch (start us, length us, event | category | flops | bytes accessed | tf_op | source)
XLA Modules:
  0.0 54.5 jit_solution(14119449503931283617)
XLA Ops:
  0.6 53.3 %cgls.1 = (f32[16,128]{1,0:T(8,128)S(1)}, f32[1,16]{1,0:T(1,128)S(1)}, f32[16,128]{1,0:T(8,128)S(1)}) custom-call(f32[3,256]{1,0:T(4,128)} %sta_ref.1, f32[3,32768]{1,0:T(4,128)} %cel_ref.1, f32[16,16,128]{2,1,0:T(8,128)} %bitcast.6, f32[1,16]{1,0:T(1,128)} %bitcast.8, f32[16,128]{1,0:T(8,128)} %bitcast.7), custom_call_target="tpu_custom_call" | custom-call | tf_op jit(solution)/shard_map/cgls/pallas_call | solution.py:385
  53.9 0.6 %write_out.1 = (f32[16,128]{1,0:T(8,128)}, f32[1,16]{1,0:T(1,128)}, f32[16,128]{1,0:T(8,128)}) custom-call(f32[16,128]{1,0:T(8,128)S(1)} %get-tuple-element.9.model, f32[1,16]{1,0:T(1,128)S(1)} %get-tuple-element.10.res, f32[16,128]{1,0:T(8,128)S(1)} %get-tuple-element.11.search), custom_call_target="tpu_custom_call" | custom-call | tf_op jit(solution)/shard_map/write_out/pallas_call | solution.py:434

commit v4 on v3

--- a/solution.py
+++ b/solution.py
@@ -91,6 +91,9 @@
         dx, dy = d // ny % nx, d % ny
         return min(dx, nx - dx) + min(dy, ny - dy), d // (nx * ny)
 
+    def far_along_z(j):
+        return (nz // 2 + jnp.where(j % 2 == 1, 0 - (j + 1) // 2, j // 2)) % nz
+
     far_first = sorted(range(1, npl), key=plane_hops, reverse=True)
 
     def z_peer(d):
@@ -113,8 +116,8 @@
     def left(ref, sem):
         pltpu.make_async_copy(ref, ref, send.at[sem]).wait()
 
-    def over_z(buf, sem, group=None):
-        for d in sorted(range(1, nz), key=lambda d: -min(d, nz - d)):
+    def over_z(buf, sem, group=None, near=0):
+        for d in sorted(range(1, nz), key=lambda d: (min(d, nz - d) > near, -min(d, nz - d))):
             landed = None if group is None else pieces.at[group, d]
             put(buf.at[0], buf.at[d], sem, z_peer(d), landed)
 
@@ -214,7 +217,7 @@
                 )
                 return 0
 
-            lax.fori_loop(0, groups, group, 0, unroll=16)
+            lax.fori_loop(0, groups, group, 0, unroll=32)
         return [
             jnp.sum(acc[s * LANES : (s + 1) * LANES, :].T, axis=0, keepdims=True)
             for s in range(srows)
@@ -243,7 +246,7 @@
             )
 
         zero = jnp.zeros((8, LANES), jnp.float32)
-        sums = lax.fori_loop(0, groups, group, (zero,) * ROWS, unroll=16)
+        sums = lax.fori_loop(0, groups, group, (zero,) * ROWS, unroll=32)
         for t in range(ROWS):
             rs_out[k, t : t + 1, :] = jnp.sum(sums[t], axis=0, keepdims=True)
 
@@ -311,7 +314,7 @@
     spread(res)
     grad = reduce_to_owner(rs1, 3)
     g_all[0] = grad
-    over_z(g_all, 4, 1)
+    over_z(g_all, 4, 1, 1)
 
     rows = forward(taken(g_all, 1))
     grads = g_all[...]
@@ -331,18 +334,27 @@
     delta = jnp.sum(jnp.sum(dl[...], axis=0), axis=1, keepdims=True)
     alpha = gamma / delta
     grad_next = grad - alpha * turn
-    sc[0] = jnp.sum(grad_next * grad_next, axis=0, keepdims=True)
-    for dz in (*reversed(near_first), 0):
-        for d in (*far_first, 0):
-            if dz or d:
-                peer = (z + dz) % nz * npl + plane_peer(d) - z * npl
-                put(sc.at[0], sc.at[dz * npl + d], 8, peer)
+    sc[0:1, :] = jnp.sum(grad_next * grad_next, axis=0, keepdims=True)
+
+    def scalars(j, _):
+        dz = far_along_z(j)
+
+        def to(d):
+            peer = (z + dz) % nz * npl + plane_peer(d) - z * npl
+            put(sc.at[pl.ds(0, 1)], sc.at[pl.ds(dz * npl + d, 1)], 8, peer)
+
+        for d in far_first:
+            to(d)
+        pl.when(dz > 0)(lambda: to(0))
+        return 0
+
+    lax.fori_loop(0, nz, scalars, 0)
     model_out[...] = m_all[0] + alpha * grad
     res_next = jnp.where(mine, res - alpha * image, 0.0)
     pad[0:1, :] = jnp.sum(res_next, axis=0, keepdims=True)
     res_out[...] = pltpu.roll(pad[...], (LANES - first % LANES) % LANES, 1)[0:1, :own_len]
     arrived(others(sc), 8)
-    gamma_next = jnp.sum(jnp.sum(sc[...], axis=0), axis=1, keepdims=True)
+    gamma_next = jnp.sum(jnp.sum(sc[...], axis=0, keepdims=True), axis=1, keepdims=True)
     search_out[...] = grad_next + gamma_next / gamma * grad
 
     left(other, 0)
@@ -411,7 +423,7 @@
                 pltpu.VMEM((npl, srows + 1, LANES), f32),
                 pltpu.VMEM((nz, 1, LANES), f32),
                 cells,
-                pltpu.VMEM((nz * npl, 1, LANES), f32),
+                pltpu.VMEM((nz * npl, LANES), f32),
                 pltpu.VMEM((8, LANES), f32),
                 pltpu.SemaphoreType.DMA((10,)),
                 pltpu.SemaphoreType.DMA((10,)),

time: 54.7 us -> 54.4 us (level)
  no operation moved by 1% of the time
where the time goes in v4:
time: 54.4 us; the launch traced here: 54.3 us
  Pallas kernels  53.5 us (98%)
  between operations  0.8 us (1%)
    pallas_call x1, Pallas kernels, per_device(): pl.pallas_call(functools.partial(body, nz, nx, ny, half, own_len, scale),...  52.8 us

profile of v4, /device:TPU:1, one launch (start us, length us, event | category | flops | bytes accessed | tf_op | source)
XLA Modules:
  0.0 54.3 jit_solution(4449451198499663148)
XLA Ops:
  0.6 52.8 %cgls.1 = (f32[16,128]{1,0:T(8,128)S(1)}, f32[1,16]{1,0:T(1,128)S(1)}, f32[16,128]{1,0:T(8,128)S(1)}) custom-call(f32[3,256]{1,0:T(4,128)} %sta_ref.1, f32[3,32768]{1,0:T(4,128)} %cel_ref.1, f32[16,16,128]{2,1,0:T(8,128)} %bitcast.6, f32[1,16]{1,0:T(1,128)} %bitcast.8, f32[16,128]{1,0:T(8,128)} %bitcast.7), custom_call_target="tpu_custom_call" | custom-call | tf_op jit(solution)/shard_map/cgls/pallas_call | solution.py:397
  53.5 0.6 %write_out.1 = (f32[16,128]{1,0:T(8,128)}, f32[1,16]{1,0:T(1,128)}, f32[16,128]{1,0:T(8,128)}) custom-call(f32[16,128]{1,0:T(8,128)S(1)} %get-tuple-element.9.model, f32[1,16]{1,0:T(1,128)S(1)} %get-tuple-element.10.res, f32[16,128]{1,0:T(8,128)S(1)} %get-tuple-element.11.search), custom_call_target="tpu_custom_call" | custom-call | tf_op jit(solution)/shard_map/write_out/pallas_call | solution.py:446

commit v5 on v4

--- a/solution.py
+++ b/solution.py
@@ -15,6 +15,7 @@
 CELL_STA = ("cell_0", "cell_1", "sta_0", "sta_1")
 
 SOFT = 0.0001
+WIDE = 512
 MID_XY = 0.5
 MID_Z = -0.275
 LANES = 128
@@ -47,8 +48,6 @@
     tile,
     lhs,
     rhs,
-    near,
-    far,
     x_pad,
     z_col,
     acc,
@@ -181,22 +180,22 @@
         ]
         rhs[k] = jnp.concatenate(parts, axis=0).astype(jnp.bfloat16)
 
-    def distances(k, base, buf):
-        buf[...] = jnp.dot(lhs[pl.ds(base, half), :], rhs[k], preferred_element_type=jnp.float32)
-
-    def kernel_of(k, base, buf):
-        for t in range(ROWS):
-            lanes = slice(t * LANES, (t + 1) * LANES)
-            dz = z_col[pl.ds(base, half), :] - cel[k, 2:3, lanes]
-            inv = lax.rsqrt(buf[:, lanes])
-            tile[k, pl.ds(base, half), lanes] = (dz * inv) * (inv * inv)
-
-    def generate(base, first, count, after):
-        bufs = (near, far)
+    def kernel_of(k, base):
+        for n in range(0, PIECE, WIDE):
+            d2 = jnp.dot(
+                lhs[pl.ds(base, half), :],
+                rhs[k, :, n : n + WIDE],
+                preferred_element_type=jnp.float32,
+            )
+            for t in range(0, WIDE, LANES):
+                lanes = slice(n + t, n + t + LANES)
+                dz = z_col[pl.ds(base, half), :] - cel[k, 2:3, lanes]
+                inv = lax.rsqrt(d2[:, t : t + LANES])
+                tile[k, pl.ds(base, half), lanes] = (dz * inv) * (inv * inv)
+
+    def generate(base, first, count):
         for i in range(count):
-            ahead = (first + i + 1, base) if i < count - 1 else after
-            distances(*ahead, bufs[(i + 1) % 2])
-            kernel_of(first + i, base, bufs[i % 2])
+            kernel_of(first + i, base)
 
     near_first = sorted(range(1, nz), key=lambda d: min(d, nz - d))
 
@@ -277,27 +276,21 @@
     for copy in loads[: 1 + nz]:
         copy.wait()
     station_side(sta, base)
-    cell_side(0)
-    distances(0, base, near)
-    for k in range(1, nz):
+    for k in range(nz):
         cell_side(k)
-    generate(base, 0, nz // 2, (nz // 2, base))
+    generate(base, 0, nz // 2)
     for copy in loads[1 + nz :]:
         copy.wait()
     pl.semaphore_wait(barrier, npl - 1 + nz - 1)
     put(sta, other, 0, plane_peer(nx * ny))
     over_z(m_all, 1, 0)
     base_2 = pl.multiple_of((1 - core) * half, half)
-    generate(base, nz // 2, nz // 4, (nz // 2 + nz // 4, base))
+    generate(base, nz // 2, nz // 2)
     arrived(other, 0)
     station_side(other, base_2)
-    generate(base, nz // 2 + nz // 4, nz // 4, (0, base_2))
-
-    def half_of(j, _):
-        generate(base_2, j * (nz // 2), nz // 2, ((j + 1) % 2 * (nz // 2), base_2))
-        return 0
-
-    lax.fori_loop(0, 2, half_of, 0)
+
+    generate(base_2, 0, nz // 2)
+    pl.when(me >= 0)(lambda: generate(base_2, nz // 2, nz // 2))
     w_all[...] = w_all[...] * scale
 
     image = jnp.concatenate(forward(taken(m_all, 0)), axis=0)
@@ -403,8 +396,6 @@
                 pltpu.VMEM((nz, stations, PIECE), f32),
                 pltpu.VMEM((stations, 32), jnp.bfloat16),
                 pltpu.VMEM((nz, 32, PIECE), jnp.bfloat16),
-                pltpu.VMEM((half, PIECE), f32),
-                pltpu.VMEM((half, PIECE), f32),
                 pltpu.VMEM((2, 8, PIECE), f32),
                 pltpu.VMEM((stations, LANES), f32),
                 pltpu.VMEM((stations, LANES), f32),

time: 54.4 us -> 54.8 us (level)
  no operation moved by 1% of the time
where the time goes in v5:
time: 54.8 us; the launch traced here: 54.6 us
  Pallas kernels  53.8 us (98%)
  between operations  0.8 us (1%)
    pallas_call x1, Pallas kernels, per_device(): pl.pallas_call(functools.partial(body, nz, nx, ny, half, own_len, scale),...  53.2 us

profile of v5, /device:TPU:1, one launch (start us, length us, event | category | flops | bytes accessed | tf_op | source)
XLA Modules:
  0.0 54.6 jit_solution(5355727467947984859)
XLA Ops:
  0.6 53.2 %cgls.1 = (f32[16,128]{1,0:T(8,128)S(1)}, f32[1,16]{1,0:T(1,128)S(1)}, f32[16,128]{1,0:T(8,128)S(1)}) custom-call(f32[3,256]{1,0:T(4,128)} %sta_ref.1, f32[3,32768]{1,0:T(4,128)} %cel_ref.1, f32[16,16,128]{2,1,0:T(8,128)} %bitcast.6, f32[1,16]{1,0:T(1,128)} %bitcast.8, f32[16,128]{1,0:T(8,128)} %bitcast.7), custom_call_target="tpu_custom_call" | custom-call | tf_op jit(solution)/shard_map/cgls/pallas_call | solution.py:390
  53.8 0.6 %write_out.1 = (f32[16,128]{1,0:T(8,128)}, f32[1,16]{1,0:T(1,128)}, f32[16,128]{1,0:T(8,128)}) custom-call(f32[16,128]{1,0:T(8,128)S(1)} %get-tuple-element.9.model, f32[1,16]{1,0:T(1,128)S(1)} %get-tuple-element.10.res, f32[16,128]{1,0:T(8,128)S(1)} %get-tuple-element.11.search), custom_call_target="tpu_custom_call" | custom-call | tf_op jit(solution)/shard_map/write_out/pallas_call | solution.py:437

commit v6 on v4

--- a/solution.py
+++ b/solution.py
@@ -274,9 +274,10 @@
         for row in (3, 7):
             x_pad[i, row : row + 1, :] = jnp.full((1, PIECE), math.sqrt(SOFT), jnp.float32)
     base = pl.multiple_of(core * half, half)
-    for copy in loads[: 1 + nz]:
-        copy.wait()
+    loads[0].wait()
     station_side(sta, base)
+    for k in range(nz):
+        loads[1 + k].wait()
     cell_side(0)
     distances(0, base, near)
     for k in range(1, nz):
@@ -284,6 +285,13 @@
     generate(base, 0, nz // 2, (nz // 2, base))
     for copy in loads[1 + nz :]:
         copy.wait()
+    pad[...] = jnp.zeros_like(pad)
+    pad[0:1, 0:own_len] = dat[...]
+    first = q * own_len
+    mine = lax.broadcasted_iota(jnp.int32, (srows, LANES), 0) == first // LANES
+    own = pltpu.roll(pad[...], first % LANES, 1)[0:1, :]
+    p1[0] = jnp.where(mine, own, 0.0)
+    w_all[...] = w_all[...] * scale
     pl.semaphore_wait(barrier, npl - 1 + nz - 1)
     put(sta, other, 0, plane_peer(nx * ny))
     over_z(m_all, 1, 0)
@@ -298,15 +306,9 @@
         return 0
 
     lax.fori_loop(0, 2, half_of, 0)
-    w_all[...] = w_all[...] * scale
 
     image = jnp.concatenate(forward(taken(m_all, 0)), axis=0)
-    pad[...] = jnp.zeros_like(pad)
-    pad[0:1, 0:own_len] = dat[...]
-    first = q * own_len
-    mine = lax.broadcasted_iota(jnp.int32, (srows, LANES), 0) == first // LANES
-    own = pltpu.roll(pad[...], first % LANES, 1)[0:1, :]
-    p1[0] = jnp.where(mine, own, 0.0) - image
+    p1[0] = p1[0] - image
     over_plane(p1, 2)
     arrived(others(p1), 2)
     res = jnp.sum(p1[...], axis=0)

time: 54.4 us -> 54.6 us (level)
  no operation moved by 1% of the time
where the time goes in v6:
time: 54.6 us; the launch traced here: 54.4 us
  Pallas kernels  53.6 us (98%)
  between operations  0.8 us (1%)
    pallas_call x1, Pallas kernels, per_device(): pl.pallas_call(functools.partial(body, nz, nx, ny, half, own_len, scale),...  53 us

profile of v6, /device:TPU:1, one launch (start us, length us, event | category | flops | bytes accessed | tf_op | source)
XLA Modules:
  0.0 54.4 jit_solution(1094424716587575067)
XLA Ops:
  0.6 53.0 %cgls.1 = (f32[16,128]{1,0:T(8,128)S(1)}, f32[1,16]{1,0:T(1,128)S(1)}, f32[16,128]{1,0:T(8,128)S(1)}) custom-call(f32[3,256]{1,0:T(4,128)} %sta_ref.1, f32[3,32768]{1,0:T(4,128)} %cel_ref.1, f32[16,16,128]{2,1,0:T(8,128)} %bitcast.6, f32[1,16]{1,0:T(1,128)} %bitcast.8, f32[16,128]{1,0:T(8,128)} %bitcast.7), custom_call_target="tpu_custom_call" | custom-call | tf_op jit(solution)/shard_map/cgls/pallas_call | solution.py:399
  53.6 0.6 %write_out.1 = (f32[16,128]{1,0:T(8,128)}, f32[1,16]{1,0:T(1,128)}, f32[16,128]{1,0:T(8,128)}) custom-call(f32[16,128]{1,0:T(8,128)S(1)} %get-tuple-element.9.model, f32[1,16]{1,0:T(1,128)S(1)} %get-tuple-element.10.res, f32[16,128]{1,0:T(8,128)S(1)} %get-tuple-element.11.search), custom_call_target="tpu_custom_call" | custom-call | tf_op jit(solution)/shard_map/write_out/pallas_call | solution.py:448

commit v7 on v6

--- a/solution.py
+++ b/solution.py
@@ -266,10 +266,10 @@
     for copy in loads:
         copy.start()
     barrier = pltpu.get_barrier_semaphore()
-    for d in range(1, npl):
+    for d in sorted(range(1, nz), key=lambda d: -min(d, nz - d)):
+        pl.semaphore_signal(barrier, inc=1, device_id=z_peer(d), device_id_type=LOGICAL)
+    for d in far_first:
         pl.semaphore_signal(barrier, inc=1, device_id=plane_peer(d), device_id_type=LOGICAL)
-    for d in range(1, nz):
-        pl.semaphore_signal(barrier, inc=1, device_id=z_peer(d), device_id_type=LOGICAL)
     for i in range(2):
         for row in (3, 7):
             x_pad[i, row : row + 1, :] = jnp.full((1, PIECE), math.sqrt(SOFT), jnp.float32)

time: 54.6 us -> 54.1 us (level)
  no operation moved by 1% of the time
where the time goes in v7:
time: 54.1 us; the launch traced here: 53.9 us
  Pallas kernels  53.1 us (98%)
  between operations  0.8 us (1%)
    pallas_call x1, Pallas kernels, per_device(): pl.pallas_call(functools.partial(body, nz, nx, ny, half, own_len, scale),...  52.5 us

profile of v7, /device:TPU:1, one launch (start us, length us, event | category | flops | bytes accessed | tf_op | source)
XLA Modules:
  0.0 53.9 jit_solution(3581597086163967406)
XLA Ops:
  0.6 52.5 %cgls.1 = (f32[16,128]{1,0:T(8,128)S(1)}, f32[1,16]{1,0:T(1,128)S(1)}, f32[16,128]{1,0:T(8,128)S(1)}) custom-call(f32[3,256]{1,0:T(4,128)} %sta_ref.1, f32[3,32768]{1,0:T(4,128)} %cel_ref.1, f32[16,16,128]{2,1,0:T(8,128)} %bitcast.6, f32[1,16]{1,0:T(1,128)} %bitcast.8, f32[16,128]{1,0:T(8,128)} %bitcast.7), custom_call_target="tpu_custom_call" | custom-call | tf_op jit(solution)/shard_map/cgls/pallas_call | solution.py:399
  53.1 0.6 %write_out.1 = (f32[16,128]{1,0:T(8,128)}, f32[1,16]{1,0:T(1,128)}, f32[16,128]{1,0:T(8,128)}) custom-call(f32[16,128]{1,0:T(8,128)S(1)} %get-tuple-element.9.model, f32[1,16]{1,0:T(1,128)S(1)} %get-tuple-element.10.res, f32[16,128]{1,0:T(8,128)S(1)} %get-tuple-element.11.search), custom_call_target="tpu_custom_call" | custom-call | tf_op jit(solution)/shard_map/write_out/pallas_call | solution.py:448
